TPU v7x, 256 devices: a 8x8x2 block of a 8x8x16 slice. The times are simulated.
256 devices in a mesh: member: 2 (over z), graph: 64 (over y, x), chan: 2 (over core).
Axes of the slice: x: 8, y: 8, z: 2, core: 2. Of those that a mesh axis runs over, the one named last changes fastest.
The devices are a block of a 8x8x16 slice.
Arguments:
- grid_state: bfloat16 [131072, 256], P(('member', 'graph')), parts along dimension 0, may hold values from -6 to 6
- w_src: bfloat16 [256, 512], P(None, 'chan'), may hold values from -0.375 to 0.375
- bias_src: float32 [512], P('chan'), may hold values from -3 to 3
- mesh_embed: bfloat16 [40960, 512], P('graph', 'chan'), may hold values from -6 to 6
- w_node: bfloat16 [512, 512], P('chan'), may hold values from -0.25 to 0.25
- w_dec: bfloat16 [512, 256], P('chan'), may hold values from -0.125 to 0.125
- slot_src: int32 [64, 64, 128], P('graph'), may hold values from 0 to 1023, as said below
- slot_dst: int32 [64, 64, 128], P(None, 'graph'), may hold values from 0 to 639, as said below
- slot_count: int32 [64, 64], replicated, may hold values from 1 to 128, as said below
Outputs:
- grid_out: bfloat16 [131072, 256], P(('member', 'graph'), 'chan'), parts along dimension 0
There are 2 independent parts, one for each index of `member`. A program takes and returns all parts, laid end to end along the dimension named above; an argument that names none is the same for every part. Nothing has to cross between parts.
Inputs may be any that keep to these rules, and one draw needn't show every extreme that they name: `slot_src`: slots at or past the live count hold arbitrary values in the same range. `slot_dst`: slots at or past the live count hold arbitrary values in the same range. slot_count[s, d] counts the live leading slots of the 128 from shard s to shard d; in every draw some receiving shard has all 128 slots live from every sender.
All inputs are finite; a program needn't handle non-finite values.
Results may differ from a plain program's by a relative error of at most 0.0056.
Values may be sent and summed in bfloat16 or wider, within the bound.
A program may use at most 64 MiB of HBM per device.

v0:
```python
import math
import jax
import jax.numpy as jnp
from jax import lax
from jax.sharding import PartitionSpec as P


def split_up(value, dim, count):
    lengths = value.shape
    parts = value.reshape(*lengths[:dim], count, lengths[dim] // count, *lengths[dim + 1 :])
    return jnp.moveaxis(parts, dim, 0)


def sum_at_owner(value, axis, dim):
    parts = split_up(value, dim, lax.axis_size(axis))
    arrived = lax.all_to_all(parts, axis, split_axis=0, concat_axis=0, tiled=True)
    return arrived.sum(axis=0)


def edge_network(source_rows, w_src, bias_src):
    return jax.nn.silu(
        jnp.dot(source_rows, w_src, preferred_element_type=jnp.float32) + bias_src
    ).astype(jnp.bfloat16)


def segment_rows(values, indices, usable, row_count):
    slot_total = values.shape[0]
    width = values.shape[1]
    block_len = math.gcd(slot_total, 2048)
    block_count = slot_total // block_len
    targets = jnp.where(usable, indices, -1).reshape(block_count, block_len)
    pieces = values.reshape(block_count, block_len, width)
    row_ids = jnp.arange(row_count, dtype=jnp.int32)

    def add_block(summed, scan_item):
        row_target, piece_vals = scan_item
        one_hot = (row_ids[:, None] == row_target[None, :]).astype(jnp.bfloat16)
        return (summed + jnp.dot(one_hot, piece_vals, preferred_element_type=jnp.float32), None)

    result, unused = lax.scan(
        add_block, jnp.zeros((row_count, width), jnp.float32), (targets, pieces)
    )
    return result


def on_device(
    grid_state, w_src, bias_src, mesh_embed, w_node, w_dec, slot_src, slot_dst, slot_count
):
    peers = lax.axis_size("graph")
    own_index = lax.axis_index("graph")
    core_index = lax.axis_index("chan")
    capacity = slot_src.shape[2]
    positions = jnp.arange(capacity, dtype=jnp.int32)
    grid_rows = grid_state.shape[0]
    mesh_rows = mesh_embed.shape[0]
    sent_counts = lax.dynamic_slice_in_dim(slot_count, own_index, 1, 0)[0]
    recv_counts = lax.dynamic_slice_in_dim(slot_count, own_index, 1, 1)[:, 0]
    half_slots = capacity // 2
    chosen = lax.dynamic_slice_in_dim(slot_src[0], core_index * half_slots, half_slots, 1)
    picked = jnp.take(grid_state, chosen.reshape(-1), axis=0).reshape(
        peers, half_slots, grid_state.shape[1]
    )
    arrived = lax.all_to_all(picked, "graph", split_axis=0, concat_axis=0, tiled=True)
    joined = lax.all_gather(arrived, "chan", axis=1, tiled=True)
    messages = edge_network(joined.reshape(peers * capacity, grid_state.shape[1]), w_src, bias_src)
    arrive_ok = (positions[None, :] < recv_counts[:, None]).reshape(-1)
    dst_rows = slot_dst[:, 0, :].reshape(-1)
    aggregate = segment_rows(messages, dst_rows, arrive_ok, mesh_rows)
    partial_hidden = jnp.dot(
        aggregate.astype(jnp.bfloat16), w_node, preferred_element_type=jnp.float32
    )
    hidden_pre = sum_at_owner(partial_hidden, "chan", 1)
    latent = (mesh_embed.astype(jnp.float32) + jax.nn.silu(hidden_pre)).astype(jnp.bfloat16)
    partial_proj = jnp.dot(latent, w_dec, preferred_element_type=jnp.float32)
    projected = sum_at_owner(partial_proj, "chan", 1).astype(jnp.bfloat16)
    returned = jnp.take(projected, dst_rows, axis=0).reshape(peers, capacity, projected.shape[1])
    came_back = lax.all_to_all(returned, "graph", split_axis=0, concat_axis=0, tiled=True).reshape(
        peers * capacity, projected.shape[1]
    )
    send_ok = (positions[None, :] < sent_counts[:, None]).reshape(-1)
    decoded = segment_rows(came_back, slot_src[0].reshape(-1), send_ok, grid_rows)
    width_half = decoded.shape[1]
    own_cols = lax.dynamic_slice_in_dim(grid_state, core_index * width_half, width_half, 1)
    return (own_cols.astype(jnp.float32) + decoded).astype(jnp.bfloat16)


def solution(mesh):
    placed = (
        P(("member", "graph"), None),
        P(None, "chan"),
        P("chan"),
        P("graph", "chan"),
        P("chan", None),
        P("chan", None),
        P("graph", None, None),
        P(None, "graph", None),
        P(),
    )
    return jax.shard_map(
        on_device,
        mesh=mesh,
        in_specs=placed,
        out_specs=P(("member", "graph"), "chan"),
        check_vma=False,
    )
```

profile of v0, /device:TPU:514, one launch (start us, length us, event | category | flops | bytes accessed | tf_op | source)
XLA Modules:
  0.0 256.0 jit_solution(5669027712290382553)
XLA Ops:
  6.5 0.0 copy-start
  6.6 0.0 all-gather.2.cloned.1.call-start
  6.6 0.9 compare_and_fusion
  7.4 0.1 reshape.128
  7.6 14.1 %gather_fusion = bf16[4096,256]{1,0:T(8,128)(2,1)S(1)} fusion(bf16[1024,256]{1,0:T(8,128)(2,1)} %param.13, s32[4096]{0:T(1024)S(1)} %broadcast_clamp_fusion.1), kind=kCustom, calls=%fused_computation | custom fusion | bytes 4210688 | tf_op jit(solution)/shard_map/jit(_take)/gather | solution.py:60
  21.7 0.8 broadcast_select_fusion
  22.5 72.0 %all_to_all.20 = bf16[64,64,256]{2,1,0:T(8,128)(2,1)} all-to-all(bf16[64,64,256]{2,1,0:T(8,128)(2,1)S(1)} %broadcast_select_fusion), channel_id=1, replica_groups=mesh['member'=2,'graph'=64,'chan'=2] {'graph'}, dimensions={0} | all-to-all | bytes 4194304 | tf_op jit(solution)/shard_map/all_to_all | solution.py:63
  94.5 0.0 copy-start.4
  94.5 0.0 copy-start.5
  94.5 0.0 copy-start.3
  94.5 0.0 copy-start.2
  94.5 0.0 copy-start.6
  94.5 0.0 copy-start.8
  94.5 0.1 all-gather.2.cloned.1.call-update
  94.6 0.7 copy-done.4
  95.3 0.0 copy-done.5
  95.3 0.1 lt.111
  95.4 0.2 dynamic-slice_reduce_fusion
  95.6 0.1 lt.117
  95.7 0.5 broadcast.108
  96.2 0.0 copy-done.3
  96.2 0.7 reduce.9
  96.9 0.0 copy-done.2
  97.0 0.2 copy.10
  97.2 0.1 broadcast_bitcast_fusion
  97.4 25.7 %all-gather.2.cloned.1.call-done = bf16[64,128,256]{2,1,0:T(8,128)(2,1)} async-done(((bf16[64,64,256]{2,1,0:T(8,128)(2,1)}), bf16[64,128,256]{2,1,0:T(8,128)(2,1)}) %all-gather.2.cloned.1.call-update) | async-done | bytes 4194320 | tf_op jit(solution)/shard_map/all_gather | solution.py:64
  123.0 0.0 copy-done.6
  123.0 0.0 copy-done.8
  123.0 6.1 %multiply_convert_fusion = bf16[8192,256]{1,0:T(8,128)(2,1)} fusion(bf16[8192,256]{1,0:T(8,128)(2,1)} %bitcast.64, bf16[256,256]{1,0:T(8,128)(2,1)S(1)} %copy-done.6, f32[256]{0:T(256)S(1)} %copy-done.8), kind=kOutput, calls=%fused_computation.21 | convolution fusion | flops 1086324736 | bytes 8520704 | tf_op jit(solution)/shard_map/dot_general | solution.py:22
  129.1 9.2 %while.22 = (s32[]{:T(128)}, f32[640,256]{1,0:T(8,128)S(1)}, s32[4,2048]{1,0:T(4,128)S(1)}, bf16[4,2048,256]{2,1,0:T(8,128)(2,1)}, s32[]{:T(128)}, /*index=5*/s32[]{:T(128)}) while((s32[]{:T(128)}, f32[640,256]{1,0:T(8,128)S(1)}, s32[4,2048]{1,0:T(4,128)S(1)}, bf16[4,2048,256]{2,1,0:T(8,128)(2,1)}, s32[]{:T(128)}, ...), condition=%wide.region_1.2_spmd.clone, body=%wide.region_0.1_spmd.clone.sunk | while | flops 672727040 | bytes 2384467 | solution.py:40
  129.1 2.3 fusion.32
  131.4 2.3 fusion.32
  133.8 2.3 fusion.32
  136.1 2.3 fusion.32
  138.3 0.0 copy-done
  138.4 0.4 fusion.16
  138.8 0.0 copy-start.7
  138.8 4.9 %all_to_all.21 = f32[2,640,256]{1,2,0:T(8,128)S(1)} all-to-all(f32[2,640,256]{1,2,0:T(8,128)S(1)} %bitcast.56), channel_id=1, replica_groups=mesh['member'=2,'graph'=64,'chan'=2] {'chan'}, dimensions={0} | all-to-all | bytes 2621440 | tf_op jit(solution)/shard_map/all_to_all | solution.py:16
  143.7 0.1 reduce_sum.18
  143.9 0.0 copy-done.7
  143.9 0.4 fusion.18
  144.3 4.3 %all_to_all.22 = f32[2,640,128]{1,2,0:T(8,128)S(1)} all-to-all(f32[2,640,128]{1,2,0:T(8,128)S(1)} %bitcast.58), channel_id=1, replica_groups=mesh['member'=2,'graph'=64,'chan'=2] {'chan'}, dimensions={0} | all-to-all | bytes 1310720 | tf_op jit(solution)/shard_map/all_to_all | solution.py:16
  148.6 0.2 copy.11
  148.8 24.0 %gather_fusion.1 = bf16[8192,128]{1,0:T(8,128)(2,1)S(1)} fusion(bf16[640,128]{1,0:T(8,128)(2,1)S(1)} %copy.11, s32[8192]{0:T(1024)S(1)} %broadcast_clamp_fusion), kind=kCustom, calls=%fused_computation.1 | custom fusion | bytes 4227072 | tf_op jit(solution)/shard_map/jit(_take)/gather | solution.py:76
  172.8 2.6 %broadcast_select_fusion.1 = bf16[64,128,128]{2,1,0:T(8,128)(2,1)} fusion(bf16[64,128,128]{2,1,0:T(8,128)(2,1)S(1)} %bitcast.54, pred[64,128]{1,0:T(8,128)(4,1)S(1)} %compare_and_fusion.1), kind=kLoop, calls=%fused_computation.23 | loop fusion | flops 1048576 | bytes 4202496 | tf_op jit(solution)/shard_map/jit(_take)/select_n | solution.py:76
  175.5 13.7 %all-to-all-start.3 = ((bf16[64,128,128]{2,1,0:T(8,128)(2,1)}), bf16[64,128,128]{2,1,0:T(8,128)(2,1)S(1)}, u32[]{:S(2)}, u32[]{:S(2)}) async-start(bf16[64,128,128]{2,1,0:T(8,128)(2,1)} %broadcast_select_fusion.1), calls=%async_computation.3 | async-start | bytes 4194304 | tf_op jit(solution)/shard_map/all_to_all | solution.py:77
  189.2 52.1 %all-to-all-done.3 = bf16[64,128,128]{2,1,0:T(8,128)(2,1)S(1)} async-done(((bf16[64,128,128]{2,1,0:T(8,128)(2,1)}), bf16[64,128,128]{2,1,0:T(8,128)(2,1)S(1)}, u32[]{:S(2)}, u32[]{:S(2)}) %all-to-all-start.3) | async-done | bytes 2097184 | tf_op jit(solution)/shard_map/all_to_all | solution.py:77
  241.3 0.0 copy-start.1
  241.3 7.0 %while.23 = (s32[]{:T(128)}, f32[1024,128]{1,0:T(8,128)S(1)}, s32[4,2048]{1,0:T(4,128)S(1)}, bf16[4,2048,128]{2,1,0:T(8,128)(2,1)S(1)}, s32[]{:T(128)}, /*index=5*/s32[]{:T(128)}) while((s32[]{:T(128)}, f32[1024,128]{1,0:T(8,128)S(1)}, s32[4,2048]{1,0:T(4,128)S(1)}, bf16[4,2048,128]{2,1,0:T(8,128)(2,1)S(1)}, s32[]{:T(128)}, ...), condition=%wide.region_5.6_spmd.clone, body=%wide.region_4.5_spmd.clone.sunk | while | flops 539230208 | bytes 1597527 | solution.py:40
  241.3 1.7 fusion.34
  243.1 1.7 fusion.34
  244.9 1.7 fusion.34
  246.6 1.7 fusion.34
  248.4 0.0 copy-done.1
  248.4 0.8 add_convert_fusion.1
  (21 shorter events, 0.3 us)
Async XLA Ops:
  6.5 131.8 %copy-start = (bf16[256,512]{1,0:T(8,128)(2,1)S(1)}, bf16[256,512]{1,0:T(8,128)(2,1)}, u32[]{:S(2)}) copy-start(bf16[256,512]{1,0:T(8,128)(2,1)} %param.17) | copy-start | bytes 786436
  6.6 116.5 %all-gather.2.cloned.1.call-start = ((), (), s32[]{:S(2)}) async-start(), calls=%async_computation.4 | async-start | bytes 6291456 | tf_op jit(solution)/shard_map/all_gather | solution.py:64
  94.5 0.8 copy-start.4
  94.5 0.8 copy-start.5
  94.5 1.7 copy-start.3
  94.5 2.4 copy-start.2
  94.5 28.5 %copy-start.6 = (bf16[256,256]{1,0:T(8,128)(2,1)S(1)}, bf16[256,256]{1,0:T(8,128)(2,1)}, u32[]{:S(2)}) copy-start(bf16[256,256]{1,0:T(8,128)(2,1)} %param.14) | copy-start | bytes 393220
  94.5 28.5 %copy-start.8 = (f32[256]{0:T(256)S(1)}, f32[256]{0:T(256)}, u32[]{:S(2)}) copy-start(f32[256]{0:T(256)} %param.15) | copy-start | bytes 3076
  138.8 5.1 %copy-start.7 = (bf16[256,256]{1,0:T(8,128)(2,1)S(1)}, bf16[256,256]{1,0:T(8,128)(2,1)}, u32[]{:S(2)}) copy-start(bf16[256,256]{1,0:T(8,128)(2,1)} %param.18) | copy-start | bytes 393220
  175.5 65.9 %all-to-all-start.3 = ((bf16[64,128,128]{2,1,0:T(8,128)(2,1)}), bf16[64,128,128]{2,1,0:T(8,128)(2,1)S(1)}, u32[]{:S(2)}, u32[]{:S(2)}) async-start(bf16[64,128,128]{2,1,0:T(8,128)(2,1)} %broadcast_select_fusion.1), calls=%async_computation.3 | async-start | bytes 4194304 | tf_op jit(solution)/shard_map/all_to_all | solution.py:77
  241.3 7.0 %copy-start.1 = (bf16[1024,256]{1,0:T(8,128)(2,1)S(1)}, bf16[1024,256]{1,0:T(8,128)(2,1)}, u32[]{:S(2)}) copy-start(bf16[1024,256]{1,0:T(8,128)(2,1)} %param.13) | copy-start | bytes 1572868
Sparse Core Ops, SparseCore 0:
  94.7 28.2 all-gather.1
where the time goes:
time: 257 us; the launch traced here: 256 us
  blocking collectives  81.2 us (32%)
  waiting for transfers between devices  77.9 us (30%)
  local copies, waits for them, and re-layouts  40.4 us (16%)
  matrix products  22.8 us (9%)
  starting transfers between devices  13.7 us (5%)
  between operations  13.7 us (5%)
  other arithmetic  6.13 us (2%)
    all_to_all x1, blocking collectives, on_device(): lax.all_to_all(picked, 'graph', split_axis=0, concat_axis=0, tiled=True)  72 us
    all_to_all x1, waiting for transfers between devices, on_device(): lax.all_to_all(returned, 'graph', split_axis=0, concat_axis=0, tiled=True)  52.1 us
    all_gather x1, waiting for transfers between devices, on_device(): joined = lax.all_gather(arrived, 'chan', axis=1, tiled=True)  25.7 us
    gather x1, local copies, waits for them, and re-layouts, on_device(): jnp.take(projected, dst_rows, axis=0)  24 us
    dot_general x8, matrix products, add_block(): jnp.dot(one_hot, piece_vals, preferred_element_type=jnp.float32)  15.9 us
    gather x1, local copies, waits for them, and re-layouts, on_device(): jnp.take(grid_state, chosen.reshape(-1), axis=0)  14.1 us
    all_to_all x1, starting transfers between devices, on_device(): lax.all_to_all(returned, 'graph', split_axis=0, concat_axis=0, tiled=True)  13.7 us
    all_to_all x2, blocking collectives, sum_at_owner(): lax.all_to_all(parts, axis, split_axis=0, concat_axis=0, tiled=True)  9.21 us
  transfers between devices with their start and end apart: 2, of which 2 were waited for; matrix products, arithmetic and copies ran while one was open for 1% of the time, Pallas kernels for 0%

commit v1 on v0

--- a/solution.py
+++ b/solution.py
@@ -61,7 +61,11 @@
         peers, half_slots, grid_state.shape[1]
     )
     arrived = lax.all_to_all(picked, "graph", split_axis=0, concat_axis=0, tiled=True)
-    joined = lax.all_gather(arrived, "chan", axis=1, tiled=True)
+    size = lax.axis_size("chan")
+    repeats = [size if d == 1 else 1 for d in range(arrived.ndim)]
+    joined = lax.all_to_all(
+        jnp.tile(arrived, repeats), "chan", split_axis=1, concat_axis=1, tiled=True
+    )
     messages = edge_network(joined.reshape(peers * capacity, grid_state.shape[1]), w_src, bias_src)
     arrive_ok = (positions[None, :] < recv_counts[:, None]).reshape(-1)
     dst_rows = slot_dst[:, 0, :].reshape(-1)

time: 257 us -> 223 us (0.87)
  blocking collectives: 81.2 us -> 16.3 us
  starting transfers between devices: 13.7 us -> 33.8 us
  waiting for transfers between devices: 77.9 us -> 97.2 us
  between operations: 13.7 us -> 0.28 us
  local copies, waits for them, and re-layouts: 40.4 us -> 44.6 us
    all_to_all x1, blocking collectives: 72 us -> 7.12 us  [on_device(): lax.all_to_all(jnp.tile(arrived, repeats), 'chan', split_axis=1, concat_a...]
    all_to_all x0 -> x1, waiting for transfers between devices: none -> 45 us  [on_device(): lax.all_to_all(picked, 'graph', split_axis=0, concat_axis=0, tiled=True)]
    all_gather x1 -> x0, waiting for transfers between devices: 25.7 us -> none  [on_device(): joined = lax.all_gather(arrived, 'chan', axis=1, tiled=True)]
    all_to_all x0 -> x1, starting transfers between devices: none -> 24.4 us  [on_device(): lax.all_to_all(picked, 'graph', split_axis=0, concat_axis=0, tiled=True)]
    all_to_all x1, starting transfers between devices: 13.7 us -> 9.35 us  [on_device(): lax.all_to_all(returned, 'graph', split_axis=0, concat_axis=0, tiled=True)]
    all_to_all x0 -> x2, local copies, waits for them, and re-layouts: none -> 3.62 us  [the longest x1 2.44 us: on_device(): lax.all_to_all(jnp.tile(arrived, repeats), 'chan', split_axis=1, concat_a...]
where the time goes in v1:
time: 223 us; the launch traced here: 220 us
  waiting for transfers between devices  97.2 us (44%)
  local copies, waits for them, and re-layouts  44.6 us (20%)
  starting transfers between devices  33.8 us (15%)
  matrix products  20.7 us (9%)
  blocking collectives  16.3 us (7%)
  other arithmetic  7.02 us (3%)
    all_to_all x1, waiting for transfers between devices, on_device(): lax.all_to_all(returned, 'graph', split_axis=0, concat_axis=0, tiled=True)  52.1 us
    all_to_all x1, waiting for transfers between devices, on_device(): lax.all_to_all(picked, 'graph', split_axis=0, concat_axis=0, tiled=True)  45 us
    all_to_all x1, starting transfers between devices, on_device(): lax.all_to_all(picked, 'graph', split_axis=0, concat_axis=0, tiled=True)  24.4 us
    gather x1, local copies, waits for them, and re-layouts, on_device(): jnp.take(projected, dst_rows, axis=0)  24 us
    dot_general x8, matrix products, add_block(): jnp.dot(one_hot, piece_vals, preferred_element_type=jnp.float32)  15.9 us
    gather x1, local copies, waits for them, and re-layouts, on_device(): jnp.take(grid_state, chosen.reshape(-1), axis=0)  14.1 us
    all_to_all x1, starting transfers between devices, on_device(): lax.all_to_all(returned, 'graph', split_axis=0, concat_axis=0, tiled=True)  9.35 us
    all_to_all x2, blocking collectives, sum_at_owner(): lax.all_to_all(parts, axis, split_axis=0, concat_axis=0, tiled=True)  9.21 us
  transfers between devices with their start and end apart: 2, of which 2 were waited for; matrix products, arithmetic and copies ran while one was open for 1% of the time, Pallas kernels for 0%

profile of v1, /device:TPU:514, one launch (start us, length us, event | category | flops | bytes accessed | tf_op | source)
XLA Modules:
  0.0 220.1 jit_solution(252606315963969498)
XLA Ops:
  0.0 0.0 copy-start
  0.0 0.9 compare_and_fusion
  0.9 0.1 reshape.132
  1.0 14.1 %gather_fusion = bf16[4096,256]{1,0:T(8,128)(2,1)S(1)} fusion(bf16[1024,256]{1,0:T(8,128)(2,1)} %param.13, s32[4096]{0:T(1024)S(1)} %broadcast_clamp_fusion.1), kind=kCustom, calls=%fused_computation | custom fusion | bytes 4210688 | tf_op jit(solution)/shard_map/jit(_take)/gather | solution.py:60
  15.1 1.7 broadcast_select_fusion
  16.9 0.0 copy-start.5
  16.9 0.0 copy-start.6
  16.9 0.0 copy-start.4
  16.9 0.0 copy-start.2
  16.9 24.4 %all-to-all-start = ((bf16[64,64,256]{2,1,0:T(8,128)(2,1)}), bf16[64,64,256]{2,1,0:T(8,128)(2,1)S(1)}, u32[]{:S(2)}, u32[]{:S(2)}) async-start(bf16[64,64,256]{2,1,0:T(8,128)(2,1)} %broadcast_select_fusion), calls=%async_computation | async-start | bytes 4194304 | tf_op jit(solution)/shard_map/all_to_all | solution.py:63
  41.3 0.0 copy-done.5
  41.3 0.0 copy-done.6
  41.4 0.1 lt.111
  41.5 0.2 dynamic-slice_reduce_fusion
  41.6 0.1 lt.117
  41.7 0.5 broadcast.111
  42.3 0.0 copy-done.4
  42.3 0.7 reduce.9
  43.0 0.0 copy-done.2
  43.0 0.9 copy.13
  44.0 0.1 broadcast_bitcast_fusion
  44.1 45.0 %all-to-all-done = bf16[64,64,256]{2,1,0:T(8,128)(2,1)S(1)} async-done(((bf16[64,64,256]{2,1,0:T(8,128)(2,1)}), bf16[64,64,256]{2,1,0:T(8,128)(2,1)S(1)}, u32[]{:S(2)}, u32[]{:S(2)}) %all-to-all-start) | async-done | bytes 2097184 | tf_op jit(solution)/shard_map/all_to_all | solution.py:63
  89.2 1.2 copy.14
  90.3 0.5 tile.4
  90.9 7.1 %all_to_all.25 = bf16[64,128,256]{2,0,1:T(8,128)(2,1)S(1)} all-to-all(bf16[64,128,256]{2,0,1:T(8,128)(2,1)S(1)} %bitcast.55), channel_id=1, replica_groups=mesh['member'=2,'graph'=64,'chan'=2] {'chan'}, dimensions={1} | all-to-all | bytes 8388608 | tf_op jit(solution)/shard_map/all_to_all | solution.py:66
  98.0 0.0 copy-start.7
  98.0 0.0 copy-start.9
  98.0 2.4 %copy.15 = bf16[64,128,256]{2,1,0:T(8,128)(2,1)S(1)} copy(bf16[64,128,256]{2,0,1:T(8,128)(2,1)S(1)} %all_to_all.25) | data formatting | bytes 8388608 | tf_op jit(solution)/shard_map/all_to_all | solution.py:66
  100.4 0.0 copy-done.7
  100.5 0.0 copy-done.9
  100.5 4.0 %multiply_convert_fusion = bf16[8192,256]{1,0:T(8,128)(2,1)} fusion(bf16[8192,256]{1,0:T(8,128)(2,1)S(1)} %bitcast.59, bf16[256,256]{1,0:T(8,128)(2,1)S(1)} %copy-done.7, f32[256]{0:T(256)S(1)} %copy-done.9), kind=kOutput, calls=%fused_computation.21 | convolution fusion | flops 1086324736 | bytes 8520704 | tf_op jit(solution)/shard_map/dot_general | solution.py:22
  104.4 9.2 %while.22 = (s32[]{:T(128)}, f32[640,256]{1,0:T(8,128)S(1)}, s32[4,2048]{1,0:T(4,128)S(1)}, bf16[4,2048,256]{2,1,0:T(8,128)(2,1)}, s32[]{:T(128)}, /*index=5*/s32[]{:T(128)}) while((s32[]{:T(128)}, f32[640,256]{1,0:T(8,128)S(1)}, s32[4,2048]{1,0:T(4,128)S(1)}, bf16[4,2048,256]{2,1,0:T(8,128)(2,1)}, s32[]{:T(128)}, ...), condition=%wide.region_1.2_spmd.clone, body=%wide.region_0.1_spmd.clone.sunk | while | flops 672727040 | bytes 2384467 | solution.py:40
  104.4 2.3 %fusion.32 = f32[640,256]{1,0:T(8,128)S(1)} fusion(s32[2048]{0:T(1024)S(1)} %bitcast.63, bf16[4,2048,256]{2,1,0:T(8,128)(2,1)} %get-tuple-element.182, s32[]{:T(128)} %get-tuple-element.173, f32[640,256]{1,0:T(8,128)S(1)} %get-tuple-element.174, pred[]{:T(512)S(6)} %compare.6), kind=kOutput, calls=%fused_computation.7.clone.1 | convolution fusion | flops 672727040 | bytes 2368001 | tf_op jit(solution)/shard_map/while/body/eval_jaxpr/dot_general | solution.py:38
  106.8 2.3 %fusion.32 = f32[640,256]{1,0:T(8,128)S(1)} fusion(s32[2048]{0:T(1024)S(1)} %bitcast.63, bf16[4,2048,256]{2,1,0:T(8,128)(2,1)} %get-tuple-element.182, s32[]{:T(128)} %get-tuple-element.173, f32[640,256]{1,0:T(8,128)S(1)} %get-tuple-element.174, pred[]{:T(512)S(6)} %compare.6), kind=kOutput, calls=%fused_computation.7.clone.1 | convolution fusion | flops 672727040 | bytes 2368001 | tf_op jit(solution)/shard_map/while/body/eval_jaxpr/dot_general | solution.py:38
  109.1 2.3 %fusion.32 = f32[640,256]{1,0:T(8,128)S(1)} fusion(s32[2048]{0:T(1024)S(1)} %bitcast.63, bf16[4,2048,256]{2,1,0:T(8,128)(2,1)} %get-tuple-element.182, s32[]{:T(128)} %get-tuple-element.173, f32[640,256]{1,0:T(8,128)S(1)} %get-tuple-element.174, pred[]{:T(512)S(6)} %compare.6), kind=kOutput, calls=%fused_computation.7.clone.1 | convolution fusion | flops 672727040 | bytes 2368001 | tf_op jit(solution)/shard_map/while/body/eval_jaxpr/dot_general | solution.py:38
  111.4 2.3 %fusion.32 = f32[640,256]{1,0:T(8,128)S(1)} fusion(s32[2048]{0:T(1024)S(1)} %bitcast.63, bf16[4,2048,256]{2,1,0:T(8,128)(2,1)} %get-tuple-element.182, s32[]{:T(128)} %get-tuple-element.173, f32[640,256]{1,0:T(8,128)S(1)} %get-tuple-element.174, pred[]{:T(512)S(6)} %compare.6), kind=kOutput, calls=%fused_computation.7.clone.1 | convolution fusion | flops 672727040 | bytes 2368001 | tf_op jit(solution)/shard_map/while/body/eval_jaxpr/dot_general | solution.py:38
  113.7 0.0 copy-done
  113.7 0.4 fusion.16
  114.1 0.0 copy-start.3
  114.1 0.0 copy-start.8
  114.1 4.9 %all_to_all.26 = f32[2,640,256]{1,2,0:T(8,128)S(1)} all-to-all(f32[2,640,256]{1,2,0:T(8,128)S(1)} %bitcast.58), channel_id=1, replica_groups=mesh['member'=2,'graph'=64,'chan'=2] {'chan'}, dimensions={0} | all-to-all | bytes 2621440 | tf_op jit(solution)/shard_map/all_to_all | solution.py:16
  119.0 0.1 reduce_sum.18
  119.2 0.0 copy-done.3
  119.2 0.0 copy-done.8
  119.2 0.4 fusion.18
  119.6 4.3 %all_to_all.27 = f32[2,640,128]{1,2,0:T(8,128)S(1)} all-to-all(f32[2,640,128]{1,2,0:T(8,128)S(1)} %bitcast.61), channel_id=1, replica_groups=mesh['member'=2,'graph'=64,'chan'=2] {'chan'}, dimensions={0} | all-to-all | bytes 1310720 | tf_op jit(solution)/shard_map/all_to_all | solution.py:16
  124.0 0.2 copy.16
  124.1 24.0 %gather_fusion.1 = bf16[8192,128]{1,0:T(8,128)(2,1)S(1)} fusion(bf16[640,128]{1,0:T(8,128)(2,1)S(1)} %copy.16, s32[8192]{0:T(1024)S(1)} %broadcast_clamp_fusion), kind=kCustom, calls=%fused_computation.1 | custom fusion | bytes 4227072 | tf_op jit(solution)/shard_map/jit(_take)/gather | solution.py:80
  148.2 2.6 %broadcast_select_fusion.1 = bf16[64,128,128]{2,1,0:T(8,128)(2,1)} fusion(bf16[64,128,128]{2,1,0:T(8,128)(2,1)S(1)} %bitcast.56, pred[64,128]{1,0:T(8,128)(4,1)S(1)} %compare_and_fusion.1), kind=kLoop, calls=%fused_computation.23 | loop fusion | flops 1048576 | bytes 4202496 | tf_op jit(solution)/shard_map/jit(_take)/select_n | solution.py:80
  150.8 9.3 %all-to-all-start.4 = ((bf16[64,128,128]{2,1,0:T(8,128)(2,1)}), bf16[64,128,128]{2,1,0:T(8,128)(2,1)S(1)}, u32[]{:S(2)}, u32[]{:S(2)}) async-start(bf16[64,128,128]{2,1,0:T(8,128)(2,1)} %broadcast_select_fusion.1), calls=%async_computation.4 | async-start | bytes 4194304 | tf_op jit(solution)/shard_map/all_to_all | solution.py:81
  160.2 52.1 %all-to-all-done.4 = bf16[64,128,128]{2,1,0:T(8,128)(2,1)S(1)} async-done(((bf16[64,128,128]{2,1,0:T(8,128)(2,1)}), bf16[64,128,128]{2,1,0:T(8,128)(2,1)S(1)}, u32[]{:S(2)}, u32[]{:S(2)}) %all-to-all-start.4) | async-done | bytes 2097184 | tf_op jit(solution)/shard_map/all_to_all | solution.py:81
  212.3 0.0 copy-start.1
  212.3 7.0 %while.23 = (s32[]{:T(128)}, f32[1024,128]{1,0:T(8,128)S(1)}, s32[4,2048]{1,0:T(4,128)S(1)}, bf16[4,2048,128]{2,1,0:T(8,128)(2,1)S(1)}, s32[]{:T(128)}, /*index=5*/s32[]{:T(128)}) while((s32[]{:T(128)}, f32[1024,128]{1,0:T(8,128)S(1)}, s32[4,2048]{1,0:T(4,128)S(1)}, bf16[4,2048,128]{2,1,0:T(8,128)(2,1)S(1)}, s32[]{:T(128)}, ...), condition=%wide.region_5.6_spmd.clone, body=%wide.region_4.5_spmd.clone.sunk | while | flops 539230208 | bytes 1597527 | solution.py:40
  212.3 1.7 fusion.34
  214.1 1.7 fusion.34
  215.9 1.7 fusion.34
  217.6 1.7 fusion.34
  219.3 0.0 copy-done.1
  219.4 0.8 add_convert_fusion.1
  (21 shorter events, 0.3 us)
Async XLA Ops:
  0.0 113.7 %copy-start = (bf16[256,512]{1,0:T(8,128)(2,1)S(1)}, bf16[256,512]{1,0:T(8,128)(2,1)}, u32[]{:S(2)}) copy-start(bf16[256,512]{1,0:T(8,128)(2,1)} %param.17) | copy-start | bytes 786436
  16.9 24.5 %copy-start.5 = (s32[1,64,128]{2,1,0:T(8,128)S(1)}, s32[1,64,128]{2,1,0:T(8,128)}, u32[]{:S(2)}) copy-start(s32[1,64,128]{2,1,0:T(8,128)} %param.19) | copy-start | bytes 98308
  16.9 24.5 %copy-start.6 = (s32[64,64]{1,0:T(8,128)S(1)}, s32[64,64]{1,0:T(8,128)}, u32[]{:S(2)}) copy-start(s32[64,64]{1,0:T(8,128)} %param.21) | copy-start | bytes 49156
  16.9 25.4 %copy-start.4 = (s32[64,1,128]{2,1,0:T(1,128)S(1)}, s32[64,1,128]{2,1,0:T(1,128)}, u32[]{:S(2)}) copy-start(s32[64,1,128]{2,1,0:T(1,128)} %param.20) | copy-start | bytes 98308
  16.9 26.1 %copy-start.2 = (bf16[640,256]{1,0:T(8,128)(2,1)S(1)}, bf16[640,256]{1,0:T(8,128)(2,1)}, u32[]{:S(2)}) copy-start(bf16[640,256]{1,0:T(8,128)(2,1)} %param.16) | copy-start | bytes 983044
  16.9 72.3 %all-to-all-start = ((bf16[64,64,256]{2,1,0:T(8,128)(2,1)}), bf16[64,64,256]{2,1,0:T(8,128)(2,1)S(1)}, u32[]{:S(2)}, u32[]{:S(2)}) async-start(bf16[64,64,256]{2,1,0:T(8,128)(2,1)} %broadcast_select_fusion), calls=%async_computation | async-start | bytes 4194304 | tf_op jit(solution)/shard_map/all_to_all | solution.py:63
  98.0 2.4 %copy-start.7 = (bf16[256,256]{1,0:T(8,128)(2,1)S(1)}, bf16[256,256]{1,0:T(8,128)(2,1)}, u32[]{:S(2)}) copy-start(bf16[256,256]{1,0:T(8,128)(2,1)} %param.14) | copy-start | bytes 393220
  98.0 2.5 %copy-start.9 = (f32[256]{0:T(256)S(1)}, f32[256]{0:T(256)}, u32[]{:S(2)}) copy-start(f32[256]{0:T(256)} %param.15) | copy-start | bytes 3076
  114.1 5.1 %copy-start.3 = (bf16[640,256]{0,1:T(8,128)(2,1)S(1)}, bf16[640,256]{0,1:T(8,128)(2,1)}, u32[]{:S(2)}) copy-start(bf16[640,256]{0,1:T(8,128)(2,1)} %copy.13) | copy-start | bytes 983044
  114.1 5.1 %copy-start.8 = (bf16[256,256]{1,0:T(8,128)(2,1)S(1)}, bf16[256,256]{1,0:T(8,128)(2,1)}, u32[]{:S(2)}) copy-start(bf16[256,256]{1,0:T(8,128)(2,1)} %param.18) | copy-start | bytes 393220
  150.8 61.5 %all-to-all-start.4 = ((bf16[64,128,128]{2,1,0:T(8,128)(2,1)}), bf16[64,128,128]{2,1,0:T(8,128)(2,1)S(1)}, u32[]{:S(2)}, u32[]{:S(2)}) async-start(bf16[64,128,128]{2,1,0:T(8,128)(2,1)} %broadcast_select_fusion.1), calls=%async_computation.4 | async-start | bytes 4194304 | tf_op jit(solution)/shard_map/all_to_all | solution.py:81
  212.3 7.0 %copy-start.1 = (bf16[1024,256]{1,0:T(8,128)(2,1)S(1)}, bf16[1024,256]{1,0:T(8,128)(2,1)}, u32[]{:S(2)}) copy-start(bf16[1024,256]{1,0:T(8,128)(2,1)} %param.13) | copy-start | bytes 1572868
